TPU v7x, 256 devices: a whole 4x4x8 slice. The times are simulated.
256 devices in a mesh: stream: 64 (over x, z, y_hi), span: 4 (over y_lo, core).
Axes of the slice: x: 4, y: 4 (y_hi: 2, y_lo: 2; y = y_hi * 2 + y_lo), z: 8, core: 2. Of those that a mesh axis runs over, the one named last changes fastest.
Arguments:
- state: float32 [2560, 8, 625], P('stream', 'span'), may hold values from -0.25 to 2.5, as said below
- direction: float32 [2560, 8, 625], P('stream', 'span'), may hold values from -6 to 6
- metric: float32 [2560, 8, 3], P('stream', 'span'), may hold values from 1 to 4
- face_source: int32 [2560, 4], P('stream'), may hold values from -1 to 225, as said below
- send_rows: int32 [64, 2, 33], P('stream'), may hold values from 0 to 159, as said below
Outputs:
- residual: float32 [2560, 8, 625], P('stream', 'span')
- basis_next: float32 [2560, 8, 625], P('stream', 'span')
- krylov: float32 [3], replicated
Inputs may be any that keep to these rules, and one draw needn't show every extreme that they name: `state`: conserved variables from density 0.75 to 1.25, flow-wise velocity 0.1 to 0.5, other velocities -0.2 to 0.2, pressure 0.5 to 0.9, so pressure and temperature are positive. `face_source`: the plane is a grid of columns of 32 cells, numbered column by column, partition d owning cells d * 40 to (d + 1) * 40 - 1 in a random local order; flow-wise faces wrap around. Every face neighbour lies in the same or an adjacent partition; -1 stands exactly on the lower face of the lowest and the upper face of the highest row; indices into received blocks point at used slots. `send_rows`: at most 33 faces per neighbouring pair, and some pair uses all 33; slots beyond a pair's count hold 0; the order of slots is the order in which the receiver's face_source refers to them.
All inputs are finite; a program needn't handle non-finite values.
Results may differ from a plain program's by a relative error of at most 0.0003.
Values sent between devices are 32-bit elements.
No kernel may reach another device: no remote copies, remote signals or barrier semaphores. Data moves between devices by JAX's collectives and lax.ppermute only.
A program may use at most 128 MiB of HBM per device.

v0:
```python
import math

import jax
import jax.numpy as jnp
import numpy as np
from jax import lax
from jax.experimental import pallas as pl
from jax.experimental.pallas import tpu as pltpu
from jax.sharding import PartitionSpec as P

GAMMA = 1.4
VISC = 0.01
COND = VISC * GAMMA / ((GAMMA - 1.0) * 0.72)
HALF_LIFT = 5.0
F32 = jnp.float32
BF16 = jnp.bfloat16

C = 40
L = 2
R = C * L
SLOTS = 33
KCAT = 256
ROW_A = 4 * C
ROW_B = 5 * C


def diff_table():
    spread = math.sqrt(3.0 / 7.0)
    points = np.array([-1.0, -spread, 0.0, spread, 1.0])
    weights = np.array([np.prod([points[i] - points[j] for j in range(5) if j != i]) for i in range(5)])
    matrix = np.zeros((5, 5))
    for i in range(5):
        for j in range(5):
            if i != j:
                matrix[i, j] = weights[i] / (weights[j] * (points[i] - points[j]))
        matrix[i, i] = np.sum([1.0 / (points[i] - points[j]) for j in range(5) if j != i])
    return matrix


def face_nodes(face):
    axis, end = face // 2, 4 * (face % 2)
    grid = np.arange(125).reshape(5, 5, 5)
    return np.take(grid, end, axis=axis).reshape(-1)


def face_lane(face):
    return face * 25 if face < 4 else 128 + (face - 4) * 25


def tables():
    d = diff_table().astype(np.float32).astype(np.float64)
    eye = np.eye(5)
    sel = np.zeros((128, 256))
    for lane in list(range(100, 128)) + list(range(178, 256)):
        sel[0, lane] = 1.0
    sel_dir = np.zeros((3, 128, 256))
    lift = np.zeros((256, 3, 128))
    d_lift = np.zeros((3, 128, 128))
    kron = [np.kron(np.kron(d, eye), eye), np.kron(np.kron(eye, d), eye), np.kron(np.kron(eye, eye), d)]
    for a in range(3):
        d_lift[a, :125, :125] = kron[a].T
        for side in range(2):
            face = 2 * a + side
            sign = 2.0 * side - 1.0
            for n, node in enumerate(face_nodes(face)):
                lane = face_lane(face) + n
                sel[node, lane] = 1.0
                sel_dir[a, node, lane] = 1.0
                lift[lane, a, node] = HALF_LIFT * sign
                d_lift[a, node, node] -= HALF_LIFT * sign
    grad_xy = np.zeros((256, 256))
    grad_z = np.zeros((256, 128))
    for a in range(2):
        grad_xy[:128, a * 128 : (a + 1) * 128] = d_lift[a]
        grad_xy[128:, a * 128 : (a + 1) * 128] = lift[:128, a]
    grad_z[:128] = d_lift[2]
    grad_z[128:] = lift[128:, 2]
    scatter = (lift != 0).sum(axis=1).astype(np.float64)

    def halves(x):
        high = x.astype(jnp.bfloat16)
        low = (x - high.astype(np.float64)).astype(jnp.bfloat16)
        return high, low

    signs = np.zeros((8, 256))
    for face in range(6):
        lanes = slice(face_lane(face), face_lane(face) + 25)
        signs[0, lanes] = HALF_LIFT * (2.0 * (face % 2) - 1.0)
        signs[1, lanes] = HALF_LIFT
    return dict(
        sel=sel.astype(jnp.bfloat16),
        sel_dir=sel_dir.reshape(384, 256).astype(jnp.bfloat16),
        scatter=scatter.astype(jnp.bfloat16),
        grad_xy=halves(grad_xy),
        grad_z=halves(grad_z),
        div=halves(d_lift.reshape(384, 128)),
        signs=signs.astype(np.float32),
    )


CONST = tables()


def mm(a, b):
    return jnp.dot(a, b, preferred_element_type=F32)


def split2(x):
    high = x.astype(BF16)
    return high, (x - high.astype(F32)).astype(BF16)


def pick(x, ones, terms=3):
    total = None
    for _ in range(terms):
        part = x.astype(BF16)
        x = x - part.astype(F32)
        total = mm(part, ones) if total is None else total + mm(part, ones)
    return total


def choose(ones, x, terms=3):
    total = None
    for _ in range(terms):
        part = x.astype(BF16)
        x = x - part.astype(F32)
        total = mm(ones, part) if total is None else total + mm(ones, part)
    return total


def mm3(x, high, low):
    xh, xl = split2(x)
    return mm(xh, high) + mm(xl, high) + mm(xh, low)


def roll(x, shift):
    shift = shift % 128
    return pltpu.roll(x, shift, 1) if shift else x


class Du:
    def __init__(self, p, t):
        self.p, self.t = p, t

    def __add__(self, o):
        return Du(self.p + o.p, self.t + o.t)

    def __sub__(self, o):
        return Du(self.p - o.p, self.t - o.t)

    def __mul__(self, o):
        if isinstance(o, Du):
            return Du(self.p * o.p, self.p * o.t + self.t * o.p)
        return Du(self.p * o, self.t * o)


def primitive(u):
    inv = 1.0 / u[0].p

    def over_density(x):
        value = x.p * inv
        return Du(value, (x.t - value * u[0].t) * inv)

    vel = [over_density(u[i]) for i in (1, 2, 3)]
    kinetic = (u[1] * vel[0] + u[2] * vel[1] + u[3] * vel[2]) * 0.5
    pressure = (u[4] - kinetic) * (GAMMA - 1.0)
    return vel, pressure, over_density(pressure)


def wave_square(vel, temper):
    return vel[0] * vel[0] + vel[1] * vel[1] + vel[2] * vel[2] + temper * GAMMA


def viscous(vel, q, a):
    div = q[0][0] + q[1][1] + q[2][2]
    stress = []
    for b in range(3):
        s = q[a][b] + q[b][a]
        if b == a:
            s = s - div * (2.0 / 3.0)
        stress.append(s * VISC)
    energy = stress[0] * vel[0] + stress[1] * vel[1] + stress[2] * vel[2] + q[a][3] * COND
    return stress + [energy]


def block(start):
    return pl.ds(pl.multiple_of(start, 8), 8)


def lanes(width=128):
    return lax.broadcasted_iota(jnp.int32, (8, width), 1)


def own_keys(width):
    j = lax.broadcasted_iota(jnp.int32, (1, width), 1)
    g = (j >= C).astype(jnp.int32) + (j >= 2 * C).astype(jnp.int32) + (j >= 3 * C).astype(jnp.int32)
    return j, 4 * (j - C * g) + g


def parity(axis):
    return lax.rem(lax.axis_index(axis), 2) == 0


def fill_table(face_ref, tab_ref, count):
    lane = lanes()

    def body(cb, carry):
        for pt in range(2):
            for l in range(L):
                tiles = [face_ref[block((pt * count + v) * R + l * C + cb * 8), :128] for v in range(count)]
                for g in range(4):
                    acc = roll(tiles[0], -25 * g)
                    for v in range(1, count):
                        acc = jnp.where(lane >= 25 * v, roll(tiles[v], 25 * (v - g)), acc)
                    tab_ref[block(g * C + cb * 8), (pt * L + l) * 128 : (pt * L + l + 1) * 128] = acc
        return carry

    lax.fori_loop(0, C // 8, body, 0)


def send_parts(send_ref, face_ref, tab_ref, be_ref, bo_ref, ze_ref, zo_ref, count):
    even = parity("stream")
    low = send_ref[0, 0:1, :].astype(F32)
    up = send_ref[0, 1:2, :].astype(F32)
    first = jnp.where(even, up, low)
    second = jnp.where(even, low, up)
    diagonal = lax.broadcasted_iota(jnp.int32, (C, SLOTS), 0) == lax.broadcasted_iota(jnp.int32, (C, SLOTS), 1)
    _, keys = own_keys(4 * C)
    keys = keys.astype(F32)
    ones = []
    for row in (first, second):
        col = jnp.sum(jnp.where(diagonal, row, 0.0), axis=1, keepdims=True)
        ones.append((col == keys).astype(BF16))
    sent = choose(jnp.concatenate(ones, axis=0), tab_ref[...])
    be_ref[...] = sent[:SLOTS]
    bo_ref[...] = sent[C : C + SLOTS]
    even_z = parity("span")
    lane = lanes()

    def body(cb, carry):
        for pt in range(2):
            edge = []
            for z, l in ((0, 0), (1, L - 1)):
                tiles = [face_ref[block((pt * count + v) * R + l * C + cb * 8), 128:] for v in range(count)]
                acc = roll(tiles[0], -25 * z)
                for v in range(1, count):
                    acc = jnp.where(lane >= 25 * v, roll(tiles[v], 25 * (v - z)), acc)
                edge.append(acc)
            cols = slice(pt * 128, (pt + 1) * 128)
            ze_ref[block(cb * 8), cols] = jnp.where(even_z, edge[1], edge[0])
            zo_ref[block(cb * 8), cols] = jnp.where(even_z, edge[0], edge[1])
        return carry

    lax.fori_loop(0, C // 8, body, 0)


def fetch_outside(fs_ref, tab_ref, re_ref, ro_ref, rze_ref, rzo_ref, face_ref, cat, got, out, count, flips):
    even = parity("stream")
    j, keys = own_keys(KCAT)
    first = j - ROW_A + 4 * C
    second = j - ROW_B + 4 * C
    first = jnp.where(even, first + SLOTS, first)
    second = jnp.where(even, second, second + SLOTS)
    keys = jnp.where(j < ROW_A, keys, jnp.where(j < ROW_A + SLOTS, first, jnp.where((j >= ROW_B) & (j < ROW_B + SLOTS), second, -5)))
    ones = jnp.concatenate([(fs_ref[:, f : f + 1] == keys).astype(BF16) for f in range(4)], axis=0)
    cat[:ROW_A, :] = tab_ref[...]
    cat[ROW_A:, :] = jnp.zeros((KCAT - ROW_A, 512), F32)
    cat[ROW_A : ROW_A + SLOTS, :] = re_ref[...]
    cat[ROW_B : ROW_B + SLOTS, :] = ro_ref[...]
    got[...] = choose(ones, cat[...])
    even_z = parity("span")
    lane = lanes()

    def body(cb, carry):
        walls = [fs_ref[block(cb * 8), f : f + 1] < 0 for f in (2, 3)]
        own = (lane >= 100) | (walls[0] & (lane >= 50) & (lane < 75)) | (walls[1] & (lane >= 75))
        for pt in range(2):
            cols = slice(pt * 128, (pt + 1) * 128)
            from_e, from_o = rze_ref[block(cb * 8), cols], rzo_ref[block(cb * 8), cols]
            above = jnp.where(even_z, from_e, from_o)
            below = jnp.where(even_z, from_o, from_e)
            for l in range(L):
                tile = slice((pt * L + l) * 128, (pt * L + l + 1) * 128)
                picked = [got[block(f * C + cb * 8), tile] for f in range(4)]
                for v in range(count):
                    rows = block((pt * count + v) * R + l * C + cb * 8)
                    acc = roll(picked[0], -25 * v)
                    for f in range(1, 4):
                        acc = jnp.where(lane >= 25 * f, roll(picked[f], 25 * (f - v)), acc)
                    mine = face_ref[rows, :128]
                    out[rows, :128] = jnp.where(own, -mine if flips and v in (1, 2, 3) else mine, acc)
                    here = face_ref[rows, 128:]
                    other = face_ref[block((pt * count + v) * R + (1 - l) * C + cb * 8), 128:]
                    if l == 0:
                        lower, upper = roll(below, -25 * v), roll(other, 25)
                    else:
                        lower, upper = roll(other, -25), roll(above, 25 - 25 * v)
                    out[rows, 128:] = jnp.where(lane < 25, lower, jnp.where(lane < 50, upper, here))
        return carry

    lax.fori_loop(0, C // 8, body, 0)


def traces_kernel(state_ref, dir_ref, metric_ref, send_ref, sel_ref, u_ref, fl_ref, tab_ref, m_ref, be_ref, bo_ref, ze_ref, zo_ref, xs):
    lane = lanes()
    xs[:, 512:640] = jnp.zeros((2 * R, 128), F32)
    for pt, ref in enumerate((state_ref, dir_ref)):
        for l in range(L):
            xs[pt * R + l * C : pt * R + (l + 1) * C, 0:625] = ref[:, l, :]
    for l in range(L):
        m_ref[l * C : (l + 1) * C, 0:3] = metric_ref[:, l, :]
    for pt in range(2):

        def body(rb, carry):
            tiles = [xs[block(pt * R + rb * 8), t * 128 : (t + 1) * 128] for t in range(5)]
            for v in range(5):
                value = roll(tiles[v], 3 * v)
                if v:
                    value = jnp.where(lane < 3 * v, roll(tiles[v - 1], 3 * v), value)
                pad = 1.0 if pt == 0 and v in (0, 4) else 0.0
                u_ref[block((pt * 5 + v) * R + rb * 8), :] = jnp.where(lane < 125, value, pad)
            return carry

        lax.fori_loop(0, R // 8, body, 0)
    fl_ref[...] = pick(u_ref[...], sel_ref[...])
    fill_table(fl_ref, tab_ref, 5)
    send_parts(send_ref, fl_ref, tab_ref, be_ref, bo_ref, ze_ref, zo_ref, 5)


def load(ref, count, rows, cols):
    return [Du(ref[block(v * R + rows), cols], ref[block((count + v) * R + rows), cols]) for v in range(count)]


def store(ref, count, v, rows, cols, value):
    ref[block(v * R + rows), cols] = value.p
    ref[block((count + v) * R + rows), cols] = value.t


ALL = slice(None)


def gradient_kernel(
    fs_ref, send_ref, u_ref, fl_ref, tab_ref, m_ref, re_ref, ro_ref, rze_ref, rzo_ref,
    gxh_ref, gxl_ref, gzh_ref, gzl_ref, sd_ref,
    out_ref, q_ref, vfl_ref, vtab_ref, be_ref, bo_ref, ze_ref, zo_ref,
    cat, got, w, wo, vv,
):
    fetch_outside(fs_ref, tab_ref, re_ref, ro_ref, rze_ref, rzo_ref, fl_ref, cat, got, out_ref, 5, True)

    def fields(rb, carry):
        rows = rb * 8
        for src, dst in ((u_ref, w), (out_ref, wo)):
            vel, _, temper = primitive(load(src, 5, rows, ALL))
            for f, value in enumerate(vel + [temper]):
                store(dst, 4, f, rows, ALL, value)
        return carry

    lax.fori_loop(0, R // 8, fields, 0)
    wh, wl = split2(w[...])
    oh, ol = split2(wo[...])
    xyh = jnp.concatenate([wh, oh[:, :128]], axis=1)
    xyl = jnp.concatenate([wl, ol[:, :128]], axis=1)
    zh = jnp.concatenate([wh, oh[:, 128:]], axis=1)
    zl = jnp.concatenate([wl, ol[:, 128:]], axis=1)
    q_ref[:, :256] = mm(xyh, gxh_ref[...]) + mm(xyl, gxh_ref[...]) + mm(xyh, gxl_ref[...])
    q_ref[:, 256:] = mm(zh, gzh_ref[...]) + mm(zl, gzh_ref[...]) + mm(zh, gzl_ref[...])

    def stresses(rb, carry):
        rows = rb * 8
        vel = [Du(w[block(f * R + rows), :], w[block((4 + f) * R + rows), :]) for f in range(3)]
        q = []
        for a in range(3):
            scale = m_ref[block(rows), a : a + 1]
            q.append([d * scale for d in load(q_ref, 4, rows, slice(a * 128, (a + 1) * 128))])
        for a in range(3):
            for v, value in enumerate(viscous(vel, q, a)):
                store(vv, 4, v, rows, slice(a * 128, (a + 1) * 128), value)
        return carry

    lax.fori_loop(0, R // 8, stresses, 0)
    q_ref[...] = vv[...]
    vfl_ref[...] = pick(vv[...], sd_ref[...], 2)
    fill_table(vfl_ref, vtab_ref, 4)
    send_parts(send_ref, vfl_ref, vtab_ref, be_ref, bo_ref, ze_ref, zo_ref, 4)


def inner_kernel(u_ref, fl_ref, out_ref, vv_ref, m_ref, sg_ref, dh_ref, dl_ref, part_ref, surf_ref, ms_ref, fv):
    lane = lanes(256)

    def volume(rb, carry):
        rows = rb * 8
        u = load(u_ref, 5, rows, ALL)
        vel, pressure, _ = primitive(u)
        total = u[4] + pressure
        for a in range(3):
            cols = slice(a * 128, (a + 1) * 128)
            scale = m_ref[block(rows), a : a + 1]
            visc = load(vv_ref, 4, rows, cols)
            store(fv, 5, 0, rows, cols, u[1 + a] * scale)
            for i in range(3):
                flux = u[1 + i] * vel[a]
                if i == a:
                    flux = flux + pressure
                store(fv, 5, 1 + i, rows, cols, (flux - visc[i]) * scale)
            store(fv, 5, 4, rows, cols, (total * vel[a] - visc[3]) * scale)
        return carry

    lax.fori_loop(0, R // 8, volume, 0)
    part_ref[...] = mm3(fv[...], dh_ref[...], dl_ref[...])

    def by_lane(x, y, z):
        return jnp.where(lane < 50, x, jnp.where(lane < 128, y, z))

    def normal(vals):
        return Du(by_lane(*[d.p for d in vals]), by_lane(*[d.t for d in vals]))

    def surface(rb, carry):
        rows = rb * 8
        inner = load(fl_ref, 5, rows, ALL)
        vel, _, temper = primitive(inner)
        speed2 = wave_square(vel, temper)
        outer = load(out_ref, 5, rows, ALL)
        vel, pressure, temper = primitive(outer)
        speed2 = (speed2 + wave_square(vel, temper)) * 0.5
        root = jnp.sqrt(speed2.p)
        speed = Du(root, 0.5 * speed2.t / root)
        mface = by_lane(*[m_ref[block(rows), a : a + 1] for a in range(3)])
        lift_s = sg_ref[0:1, :] * mface
        lift = sg_ref[1:2, :] * mface
        ms_ref[block(rows), :] = lift_s
        speed = speed * lift
        vn = normal(vel)
        fluxes = [normal(outer[1:4])]
        for i in range(3):
            flux = outer[1 + i] * vn
            side = (lane < 50) if i == 0 else ((lane >= 50) & (lane < 128)) if i == 1 else (lane >= 128)
            fluxes.append(Du(flux.p + jnp.where(side, pressure.p, 0.0), flux.t + jnp.where(side, pressure.t, 0.0)))
        fluxes.append((outer[4] + pressure) * vn)
        for v in range(5):
            store(surf_ref, 5, v, rows, ALL, fluxes[v] * lift_s - speed * (outer[v] - inner[v]))
        return carry

    lax.fori_loop(0, R // 8, surface, 0)


def unpack(tiles, lane, t):
    value = roll(tiles[t], -3 * t)
    if t < 4:
        value = jnp.where(lane < 125 - 3 * t, value, roll(tiles[t + 1], -3 * (t + 1)))
    return value


def final_kernel(
    fs_ref, vtab_ref, re_ref, ro_ref, rze_ref, rzo_ref, vfl_ref, part_ref, surf_ref, ms_ref, u_ref, sc_ref,
    res_ref, prod_ref, sums_ref,
    cat, got, vo, sf, xs,
):
    fetch_outside(fs_ref, vtab_ref, re_ref, ro_ref, rze_ref, rzo_ref, vfl_ref, cat, got, vo, 4, False)

    def surface(rb, carry):
        rows = rb * 8
        scale = ms_ref[block(rows), :]
        for pt in range(2):
            sf[block(pt * 5 * R + rows), :] = surf_ref[block(pt * 5 * R + rows), :]
            for v in range(4):
                at = block((pt * 5 + 1 + v) * R + rows)
                sf[at, :] = surf_ref[at, :] - scale * vo[block((pt * 4 + v) * R + rows), :]
        return carry

    lax.fori_loop(0, R // 8, surface, 0)
    sf[:, :128] = part_ref[...] + pick(sf[...], sc_ref[...], 2)
    lane = lanes()

    def output(rb, sums):
        sums = list(sums)
        rows = rb * 8
        prod = []
        for pt in range(2):
            tiles = [sf[block((pt * 5 + v) * R + rows), :128] for v in range(5)]
            tiles = [jnp.where(lane < 125, x, 0.0) for x in tiles]
            for t in range(5):
                xs[block(pt * R + rows), t * 128 : (t + 1) * 128] = unpack(tiles, lane, t)
            prod.append(tiles)
        for v in range(5):
            d = u_ref[block((5 + v) * R + rows), :]
            res, p = prod[0][v], prod[1][v]
            for i, x in enumerate((d * p, d * d, res * res, p * p)):
                sums[i] = sums[i] + x
        return tuple(sums)

    zero = jnp.zeros((8, 128), F32)
    sums = lax.fori_loop(0, R // 8, output, (zero, zero, zero, zero))
    lane1 = lax.broadcasted_iota(jnp.int32, (1, 128), 1)
    row = jnp.zeros((1, 128), F32)
    for i, x in enumerate(sums):
        x = jnp.sum(jnp.sum(x, axis=0, keepdims=True), axis=1, keepdims=True)
        row = jnp.where(lane1 == i, x, row)
    sums_ref[...] = row
    for pt, ref in enumerate((res_ref, prod_ref)):
        for l in range(L):
            ref[:, l, :] = xs[pt * R + l * C : pt * R + (l + 1) * C, 0:625]


def scale_kernel(all_ref, prod_ref, dir_ref, basis_ref, krylov_ref, *, total):
    sums = jnp.sum(all_ref[...], axis=0, keepdims=True)
    dp, dd, rr, pp = [sums[:, i : i + 1] for i in range(4)]
    coefficient = dp / total
    beta = jnp.sqrt((pp - 2.0 * coefficient * dp + coefficient * coefficient * dd) / total)
    norm = jnp.sqrt(rr / total)
    lane1 = lax.broadcasted_iota(jnp.int32, (1, 128), 1)
    krylov_ref[...] = jnp.where(lane1 == 0, coefficient, jnp.where(lane1 == 1, beta, norm))
    basis_ref[...] = (prod_ref[...] - coefficient.reshape(1, 1, 1) * dir_ref[...]) / beta.reshape(1, 1, 1)


def shaped(*dims):
    return jax.ShapeDtypeStruct(dims, F32)


def vmem(*dims):
    return pltpu.VMEM(dims, F32)


def pairs_of(count):
    first = [(i, i ^ 1) for i in range(count)]
    second = [(i, (((i + 1) ^ 1) - 1) % count) for i in range(count)]
    return first, second


def exchange(be, bo, ze, zo):
    se, so = pairs_of(lax.axis_size("stream"))
    pe, po = pairs_of(lax.axis_size("span"))
    return (
        lax.ppermute(be, "stream", se),
        lax.ppermute(bo, "stream", so),
        lax.ppermute(ze, "span", pe),
        lax.ppermute(zo, "span", po),
    )


SENT = (shaped(SLOTS, 512), shaped(SLOTS, 512), shaped(C, 256), shaped(C, 256))


def local(state, direction, metric, face_source, send_rows):
    u, fl, tab, m, *sent = pl.pallas_call(
        traces_kernel,
        out_shape=(shaped(10 * R, 128), shaped(10 * R, 256), shaped(4 * C, 512), shaped(R, 128)) + SENT,
        scratch_shapes=[vmem(2 * R, 640)],
        name="traces",
    )(state, direction, metric, send_rows, CONST["sel"])
    got = exchange(*sent)
    out, vv, vfl, vtab, *sent = pl.pallas_call(
        gradient_kernel,
        out_shape=(shaped(10 * R, 256), shaped(8 * R, 384), shaped(8 * R, 256), shaped(4 * C, 512)) + SENT,
        scratch_shapes=[vmem(KCAT, 512), vmem(4 * C, 512), vmem(8 * R, 128), vmem(8 * R, 256), vmem(8 * R, 384)],
        name="gradient",
    )(face_source, send_rows, u, fl, tab, m, *got, *CONST["grad_xy"], *CONST["grad_z"], CONST["sel_dir"])
    got = exchange(*sent)
    part, surf, ms = pl.pallas_call(
        inner_kernel,
        out_shape=(shaped(10 * R, 128), shaped(10 * R, 256), shaped(R, 256)),
        scratch_shapes=[vmem(10 * R, 384)],
        name="inner",
    )(u, fl, out, vv, m, CONST["signs"], *CONST["div"])
    residual, product, sums = pl.pallas_call(
        final_kernel,
        out_shape=(shaped(C, L, 625), shaped(C, L, 625), shaped(1, 128)),
        scratch_shapes=[vmem(KCAT, 512), vmem(4 * C, 512), vmem(8 * R, 256), vmem(10 * R, 256), vmem(2 * R, 640)],
        name="final",
    )(face_source, vtab, *got, vfl, part, surf, ms, u, CONST["scatter"])
    axes = ("stream", "span")
    count = lax.axis_size("stream") * lax.axis_size("span")
    spread = jnp.broadcast_to(sums[None], (count, 1, 128))
    everyone = lax.all_to_all(spread, axes, 0, 0, tiled=True).reshape(count, 128)
    total = float(state.size * count)
    basis, krylov = pl.pallas_call(
        lambda *refs: scale_kernel(*refs, total=total),
        out_shape=(shaped(C, L, 625), shaped(1, 128)),
        name="scale",
    )(everyone, product, direction)
    return residual, basis, krylov[0, :3]


def solution(mesh):
    cells = P("stream", "span", None)
    in_specs = (cells, cells, cells, P("stream", None), P("stream", None, None))
    out_specs = (cells, cells, P())
    return jax.shard_map(local, mesh=mesh, in_specs=in_specs, out_specs=out_specs, check_vma=False)
```

profile of v0, /device:TPU:1, one launch (start us, length us, event | category | flops | bytes accessed | tf_op | source)
XLA Modules:
  0.0 77.0 jit_solution(12859592930541105397)
XLA Ops:
  0.6 1.4 %copy.21.metric_ref = f32[40,2,3]{2,1,0:T(2,128)} copy(f32[40,2,3]{0,1,2:T(2,128)} %param.17) | data formatting | bytes 1920 | tf_op args[2]
  2.0 5.8 %traces.1 = (f32[800,128]{1,0:T(8,128)}, f32[800,256]{1,0:T(8,128)}, f32[160,512]{1,0:T(8,128)}, f32[80,128]{1,0:T(8,128)}, f32[33,512]{1,0:T(8,128)}, /*index=5...) custom-call(f32[40,2,625]{2,1,0:T(2,128)} %state_ref.1, f32[40,2,625]{2,1,0:T(2,128)} %refs_2_.1, ...), custom_call_target="tpu_custom_call" | custom-call | tf_op jit(solution)/shard_map/traces/pallas_call | solution.py:544
  7.8 3.7 %collective-permute-start = (f32[33,512]{1,0:T(8,128)}, f32[33,512]{1,0:T(8,128)S(1)}, u32[]{:S(2)}, u32[]{:S(2)}) collective-permute-start(f32[33,512]{1,0:T(8,128)} %get-tuple-element.31), channel_id=1, source_target_pairs={{0,4},{4,0},{8,12},{12,8},{16,20},{20,16},{24,28},{28,24},{32,36},... | collective-permute-start | bytes 202760 | tf_op jit(solution)/shard_map/ppermute | solution.py:533
  11.6 0.0 copy-start.8
  11.6 7.6 %collective-permute-start.1 = (f32[33,512]{1,0:T(8,128)}, f32[33,512]{1,0:T(8,128)S(1)}, u32[]{:S(2)}, u32[]{:S(2)}) collective-permute-start(f32[33,512]{1,0:T(8,128)} %get-tuple-element.32), channel_id=1, source_target_pairs={{0,252},{4,8},{8,4},{12,16},{16,12},{20,24},{24,20},{28,32},{32,28... | collective-permute-start | bytes 202760 | tf_op jit(solution)/shard_map/ppermute | solution.py:534
  19.2 1.2 %collective-permute-start.2 = (f32[40,256]{1,0:T(8,128)}, f32[40,256]{1,0:T(8,128)S(1)}, u32[]{:S(2)}, u32[]{:S(2)}) collective-permute-start(f32[40,256]{1,0:T(8,128)} %get-tuple-element.33), channel_id=1, source_target_pairs={{0,1},{1,0},{2,3},{3,2},{4,5},{5,4},{6,7},{7,6},{8,9},{9,8},{10,11... | collective-permute-start | bytes 122888 | tf_op jit(solution)/shard_map/ppermute | solution.py:535
  20.4 1.2 %collective-permute-start.3 = (f32[40,256]{1,0:T(8,128)}, f32[40,256]{1,0:T(8,128)S(1)}, u32[]{:S(2)}, u32[]{:S(2)}) collective-permute-start(f32[40,256]{1,0:T(8,128)} %get-tuple-element.34), channel_id=1, source_target_pairs={{0,3},{1,2},{2,1},{3,0},{4,7},{5,6},{6,5},{7,4},{8,11},{9,10},{10,... | collective-permute-start | bytes 122888 | tf_op jit(solution)/shard_map/ppermute | solution.py:536
  21.5 0.0 copy-done.8
  21.6 0.7 copy.23.fs_ref
  22.2 0.0 collective-permute-done.2.rze_ref
  22.2 0.0 copy-start.6
  22.2 1.8 %collective-permute-done.3.rzo_ref = f32[40,256]{1,0:T(8,128)S(1)} collective-permute-done((f32[40,256]{1,0:T(8,128)}, f32[40,256]{1,0:T(8,128)S(1)}, u32[]{:S(2)}, u32[]{:S(2)}) %collective-permute-start.3) | collective-permute-done | bytes 40992 | tf_op jit(solution)/shard_map/ppermute | solution.py:536
  24.0 0.0 copy-start.7
  24.0 0.0 collective-permute-done.re_ref
  24.0 0.0 copy-start.2
  24.0 0.0 collective-permute-done.1.ro_ref
  24.0 0.0 copy-start.3
  24.0 0.0 copy-done.6
  24.0 0.6 copy-done.7
  24.6 0.0 copy-done.2
  24.7 0.0 copy-done.3
  24.7 8.9 %gradient.1 = (f32[800,256]{1,0:T(8,128)}, f32[640,384]{1,0:T(8,128)}, f32[640,256]{1,0:T(8,128)}, f32[160,512]{1,0:T(8,128)}, f32[33,512]{1,0:T(8,128)}, /*inde...) custom-call(s32[40,4]{1,0:T(8,128)} %copy.23.fs_ref, s32[1,2,33]{2,1,0:T(2,128)} %send_ref.3, ...), custom_call_target="tpu_custom_call" | custom-call | tf_op jit(solution)/shard_map/gradient/pallas_call | solution.py:551
  33.6 0.1 collective-permute-start.4
  33.7 4.4 %collective-permute-start.5 = (f32[33,512]{1,0:T(8,128)}, f32[33,512]{1,0:T(8,128)S(1)}, u32[]{:S(2)}, u32[]{:S(2)}) collective-permute-start(f32[33,512]{1,0:T(8,128)} %get-tuple-element.37), channel_id=1, source_target_pairs={{0,252},{4,8},{8,4},{12,16},{16,12},{20,24},{24,20},{28,32},{32,28... | collective-permute-start | bytes 202760 | tf_op jit(solution)/shard_map/ppermute | solution.py:534
  38.1 2.3 %collective-permute-start.6 = (f32[40,256]{1,0:T(8,128)}, f32[40,256]{1,0:T(8,128)S(1)}, u32[]{:S(2)}, u32[]{:S(2)}) collective-permute-start(f32[40,256]{1,0:T(8,128)} %get-tuple-element.38), channel_id=1, source_target_pairs={{0,1},{1,0},{2,3},{3,2},{4,5},{5,4},{6,7},{7,6},{8,9},{9,8},{10,11... | collective-permute-start | bytes 122888 | tf_op jit(solution)/shard_map/ppermute | solution.py:535
  40.5 1.2 %collective-permute-start.7 = (f32[40,256]{1,0:T(8,128)}, f32[40,256]{1,0:T(8,128)S(1)}, u32[]{:S(2)}, u32[]{:S(2)}) collective-permute-start(f32[40,256]{1,0:T(8,128)} %get-tuple-element.39), channel_id=1, source_target_pairs={{0,3},{1,2},{2,1},{3,0},{4,7},{5,6},{6,5},{7,4},{8,11},{9,10},{10,... | collective-permute-start | bytes 122888 | tf_op jit(solution)/shard_map/ppermute | solution.py:536
  41.6 5.2 %inner.1 = (f32[800,128]{1,0:T(8,128)}, f32[800,256]{1,0:T(8,128)}, f32[80,256]{1,0:T(8,128)}) custom-call(f32[800,128]{1,0:T(8,128)} %get-tuple-element.27.u_ref, f32[800,256]{1,0:T(8,128)} %get-tuple-element.28.fl_ref, f32[800,256]{1,0:T(8,128)} %get-tuple-element.41.out_ref, f32[640,384]{1,0:T(8,128)} %get-tuple-element.42.vv_ref, ...), custom_call_target="tpu_custom_call" | custom-call | tf_op jit(solution)/shard_map/inner/pallas_call | solution.py:558
  46.9 0.0 collective-permute-done.6.rze_ref
  46.9 0.0 copy-start.4
  46.9 0.0 collective-permute-done.7.rzo_ref
  46.9 0.0 copy-start.5
  46.9 0.0 collective-permute-done.4.re_ref
  46.9 0.0 copy-start
  46.9 0.0 collective-permute-done.5.ro_ref
  46.9 0.0 copy-start.1
  47.0 0.5 copy-done.4
  47.5 0.0 copy-done.5
  47.5 0.0 copy-done
  47.6 0.0 copy-done.1
  47.6 5.1 %final.1 = (f32[40,2,625]{2,1,0:T(2,128)}, f32[40,2,625]{2,1,0:T(2,128)}, f32[1,128]{1,0:T(1,128)}) custom-call(s32[40,4]{1,0:T(8,128)} %copy.23.fs_ref, f32[160,512]{1,0:T(8,128)} %get-tuple-element.35.vtab_ref, f32[33,512]{1,0:T(8,128)} %copy-done, f32[33,512]{1,0:T(8,128)} %copy-done.1, f32[40,256]{1,0:T(8,128)} %copy-done.4, f32[40,256]{1,0:T(8,128)} %copy-done.5, ...), custom_call_target="tpu_custom_call" | custom-call | tf_op jit(solution)/shard_map/final/pallas_call | solution.py:564
  52.7 0.0 copy-start.9
  52.7 0.7 copy-done.9
  53.4 0.1 broadcast_in_dim.9
  53.4 20.3 %all_to_all.5 = f32[256,1,128]{2,1,0:T(1,128)} all-to-all(f32[256,1,128]{2,1,0:T(1,128)S(1)} %broadcast_in_dim.9), channel_id=1, replica_groups=mesh['stream'=64,'span'=4] {'stream','span'}, dimensions={0} | all-to-all | bytes 262144 | tf_op jit(solution)/shard_map/all_to_all | solution.py:573
  73.8 2.1 %scale.1 = (f32[40,2,625]{2,1,0:T(2,128)}, f32[1,128]{1,0:T(1,128)}) custom-call(f32[256,128]{1,0:T(8,128)} %bitcast.4, f32[40,2,625]{2,1,0:T(2,128)} %get-tuple-element.48.refs_1_, f32[40,2,625]{2,1,0:T(2,128)} %refs_2_.1), custom_call_target="tpu_custom_call" | custom-call | tf_op jit(solution)/shard_map/scale/pallas_call | solution.py:575
  75.9 0.0 copy-start.10
  75.9 0.7 copy-done.10
  76.5 0.5 slice_bitcast_fusion
Async XLA Ops:
  7.8 16.2 %collective-permute-start = (f32[33,512]{1,0:T(8,128)}, f32[33,512]{1,0:T(8,128)S(1)}, u32[]{:S(2)}, u32[]{:S(2)}) collective-permute-start(f32[33,512]{1,0:T(8,128)} %get-tuple-element.31), channel_id=1, source_target_pairs={{0,4},{4,0},{8,12},{12,8},{16,20},{20,16},{24,28},{28,24},{32,36},... | collective-permute-start | bytes 202760 | tf_op jit(solution)/shard_map/ppermute | solution.py:533
  11.6 10.0 %copy-start.8 = (s32[40,4]{0,1:T(4,128)S(1)}, s32[40,4]{0,1:T(4,128)}, u32[]{:S(2)}) copy-start(s32[40,4]{0,1:T(4,128)} %param.18) | copy-start | bytes 1924
  11.6 12.4 %collective-permute-start.1 = (f32[33,512]{1,0:T(8,128)}, f32[33,512]{1,0:T(8,128)S(1)}, u32[]{:S(2)}, u32[]{:S(2)}) collective-permute-start(f32[33,512]{1,0:T(8,128)} %get-tuple-element.32), channel_id=1, source_target_pairs={{0,252},{4,8},{8,4},{12,16},{16,12},{20,24},{24,20},{28,32},{32,28... | collective-permute-start | bytes 202760 | tf_op jit(solution)/shard_map/ppermute | solution.py:534
  19.2 3.1 %collective-permute-start.2 = (f32[40,256]{1,0:T(8,128)}, f32[40,256]{1,0:T(8,128)S(1)}, u32[]{:S(2)}, u32[]{:S(2)}) collective-permute-start(f32[40,256]{1,0:T(8,128)} %get-tuple-element.33), channel_id=1, source_target_pairs={{0,1},{1,0},{2,3},{3,2},{4,5},{5,4},{6,7},{7,6},{8,9},{9,8},{10,11... | collective-permute-start | bytes 122888 | tf_op jit(solution)/shard_map/ppermute | solution.py:535
  20.4 3.6 %collective-permute-start.3 = (f32[40,256]{1,0:T(8,128)}, f32[40,256]{1,0:T(8,128)S(1)}, u32[]{:S(2)}, u32[]{:S(2)}) collective-permute-start(f32[40,256]{1,0:T(8,128)} %get-tuple-element.34), channel_id=1, source_target_pairs={{0,3},{1,2},{2,1},{3,0},{4,7},{5,6},{6,5},{7,4},{8,11},{9,10},{10,... | collective-permute-start | bytes 122888 | tf_op jit(solution)/shard_map/ppermute | solution.py:536
  22.2 1.8 %copy-start.6 = (f32[40,256]{1,0:T(8,128)}, f32[40,256]{1,0:T(8,128)S(1)}, u32[]{:S(2)}) copy-start(f32[40,256]{1,0:T(8,128)S(1)} %collective-permute-done.2.rze_ref) | copy-start | bytes 122884
  24.0 0.6 copy-start.7
  24.0 0.6 copy-start.2
  24.0 0.7 copy-start.3
  33.6 13.3 %collective-permute-start.4 = (f32[33,512]{1,0:T(8,128)}, f32[33,512]{1,0:T(8,128)S(1)}, u32[]{:S(2)}, u32[]{:S(2)}) collective-permute-start(f32[33,512]{1,0:T(8,128)} %get-tuple-element.36), channel_id=1, source_target_pairs={{0,4},{4,0},{8,12},{12,8},{16,20},{20,16},{24,28},{28,24},{32,36},... | collective-permute-start | bytes 202760 | tf_op jit(solution)/shard_map/ppermute | solution.py:533
  33.7 13.3 %collective-permute-start.5 = (f32[33,512]{1,0:T(8,128)}, f32[33,512]{1,0:T(8,128)S(1)}, u32[]{:S(2)}, u32[]{:S(2)}) collective-permute-start(f32[33,512]{1,0:T(8,128)} %get-tuple-element.37), channel_id=1, source_target_pairs={{0,252},{4,8},{8,4},{12,16},{16,12},{20,24},{24,20},{28,32},{32,28... | collective-permute-start | bytes 202760 | tf_op jit(solution)/shard_map/ppermute | solution.py:534
  38.1 8.8 %collective-permute-start.6 = (f32[40,256]{1,0:T(8,128)}, f32[40,256]{1,0:T(8,128)S(1)}, u32[]{:S(2)}, u32[]{:S(2)}) collective-permute-start(f32[40,256]{1,0:T(8,128)} %get-tuple-element.38), channel_id=1, source_target_pairs={{0,1},{1,0},{2,3},{3,2},{4,5},{5,4},{6,7},{7,6},{8,9},{9,8},{10,11... | collective-permute-start | bytes 122888 | tf_op jit(solution)/shard_map/ppermute | solution.py:535
  40.5 6.4 %collective-permute-start.7 = (f32[40,256]{1,0:T(8,128)}, f32[40,256]{1,0:T(8,128)S(1)}, u32[]{:S(2)}, u32[]{:S(2)}) collective-permute-start(f32[40,256]{1,0:T(8,128)} %get-tuple-element.39), channel_id=1, source_target_pairs={{0,3},{1,2},{2,1},{3,0},{4,7},{5,6},{6,5},{7,4},{8,11},{9,10},{10,... | collective-permute-start | bytes 122888 | tf_op jit(solution)/shard_map/ppermute | solution.py:536
  46.9 0.6 copy-start.4
  46.9 0.6 copy-start.5
  46.9 0.6 copy-start
  46.9 0.6 copy-start.1
  52.7 0.7 copy-start.9
  75.9 0.7 copy-start.10
where the time goes:
time: 77.3 us; the launch traced here: 77 us
  Pallas kernels  27.2 us (35%)
  starting transfers between devices  21.8 us (28%)
  blocking collectives  20.3 us (26%)
  local copies, waits for them, and re-layouts  5.25 us (7%)
  waiting for transfers between devices  1.78 us (2%)
    all_to_all x1, blocking collectives, local(): lax.all_to_all(spread, axes, 0, 0, tiled=True).reshape(count, 128)  20.3 us
    ppermute x2, starting transfers between devices, exchange(): lax.ppermute(bo, 'stream', so)  12 us
    pallas_call x1, Pallas kernels, local(): pl.pallas_call(gradient_kernel, out_shape=(shaped(10 * R, 256), shaped(8...  8.9 us
    pallas_call x1, Pallas kernels, local(): pl.pallas_call(traces_kernel, out_shape=(shaped(10 * R, 128), shaped(10 *...  5.83 us
    pallas_call x1, Pallas kernels, local(): pl.pallas_call(inner_kernel, out_shape=(shaped(10 * R, 128), shaped(10 *...  5.24 us
    pallas_call x1, Pallas kernels, local(): pl.pallas_call(final_kernel, out_shape=(shaped(C, L, 625), shaped(C, L, 6...  5.11 us
    unnamed x24, local copies, waits for them, and re-layouts  4.67 us
    ppermute x2, starting transfers between devices, exchange(): lax.ppermute(be, 'stream', se)  3.83 us
  transfers between devices with their start and end apart: 8, of which 1 were waited for; matrix products, arithmetic and copies ran while one was open for 1% of the time, Pallas kernels for 7%

commit v1 on v0

v1 whole, which is shorter than its diff:
```python
import math

import jax
import jax.numpy as jnp
import numpy as np
from jax import lax
from jax.experimental import pallas as pl
from jax.experimental.pallas import tpu as pltpu
from jax.sharding import PartitionSpec as P

GAMMA = 1.4
VISC = 0.01
COND = VISC * GAMMA / ((GAMMA - 1.0) * 0.72)
HALF_LIFT = 5.0
F32 = jnp.float32
BF16 = jnp.bfloat16

C = 40
L = 2
R = C * L
SLOTS = 33


def diff_table():
    spread = math.sqrt(3.0 / 7.0)
    points = np.array([-1.0, -spread, 0.0, spread, 1.0])
    weights = np.array([np.prod([points[i] - points[j] for j in range(5) if j != i]) for i in range(5)])
    matrix = np.zeros((5, 5))
    for i in range(5):
        for j in range(5):
            if i != j:
                matrix[i, j] = weights[i] / (weights[j] * (points[i] - points[j]))
        matrix[i, i] = np.sum([1.0 / (points[i] - points[j]) for j in range(5) if j != i])
    return matrix


def face_nodes(face):
    axis, end = face // 2, 4 * (face % 2)
    grid = np.arange(125).reshape(5, 5, 5)
    return np.take(grid, end, axis=axis).reshape(-1)


def face_lane(face):
    return face * 25 if face < 4 else 128 + (face - 4) * 25


def tables():
    d = diff_table().astype(np.float32).astype(np.float64)
    eye = np.eye(5)
    sel = np.zeros((128, 256))
    for lane in list(range(100, 128)) + list(range(178, 256)):
        sel[0, lane] = 1.0
    trace = np.zeros((640, 768))
    trace_v = np.zeros((3, 512, 256))
    place_v = np.zeros((768, 512))
    lift = np.zeros((256, 3, 128))
    d_lift = np.zeros((3, 128, 128))
    kron = [np.kron(np.kron(d, eye), eye), np.kron(np.kron(eye, d), eye), np.kron(np.kron(eye, eye), d)]
    signs = np.zeros((8, 256))
    for a in range(3):
        d_lift[a, :125, :125] = kron[a].T
        for side in range(2):
            face = 2 * a + side
            sign = 2.0 * side - 1.0
            signs[0, face_lane(face) : face_lane(face) + 25] = HALF_LIFT * sign
            signs[1, face_lane(face) : face_lane(face) + 25] = HALF_LIFT
            for n, node in enumerate(face_nodes(face)):
                lane = face_lane(face) + n
                sel[node, lane] = 1.0
                lift[lane, a, node] = HALF_LIFT * sign
                d_lift[a, node, node] -= HALF_LIFT * sign
                for v in range(5):
                    trace[v * 125 + node, face * 128 + v * 25 + n] = 1.0
                for v in range(4):
                    trace_v[a, v * 128 + node, side * 128 + v * 25 + n] = 1.0
                    place_v[face * 128 + v * 25 + n, v * 128 + node] = 1.0
    scatter = (lift != 0).sum(axis=1).astype(np.float64)

    def halves(x):
        high = x.astype(jnp.bfloat16)
        low = (x - high.astype(np.float64)).astype(jnp.bfloat16)
        return np.concatenate([high, low], axis=0)

    return dict(
        trace=trace.astype(jnp.bfloat16),
        sel=sel.astype(jnp.bfloat16),
        grad=halves(np.concatenate(list(d_lift), axis=1)),
        lift_xy=np.concatenate([lift[:128, 0], lift[:128, 1]], axis=1).astype(jnp.bfloat16),
        lift_z=lift[128:, 2].astype(jnp.bfloat16),
        trace_v=trace_v.reshape(1536, 256).astype(jnp.bfloat16),
        place_v=place_v.astype(jnp.bfloat16),
        scatter=scatter.astype(jnp.bfloat16),
        div=halves(d_lift.reshape(384, 128)),
        signs=signs.astype(np.float32),
    )


CONST = tables()


def mm(a, b):
    return jnp.dot(a, b, preferred_element_type=F32)


def split2(x):
    high = x.astype(BF16)
    return high, (x - high.astype(F32)).astype(BF16)


def pick(x, ones, terms=3):
    total = None
    for _ in range(terms):
        part = x.astype(BF16)
        x = x - part.astype(F32)
        total = mm(part, ones) if total is None else total + mm(part, ones)
    return total


def choose(ones, x, terms=3):
    total = None
    for _ in range(terms):
        part = x.astype(BF16)
        x = x - part.astype(F32)
        total = mm(ones, part) if total is None else total + mm(ones, part)
    return total


def mm3(x, high, low):
    xh, xl = split2(x)
    return mm(xh, high) + mm(xl, high) + mm(xh, low)


def roll(x, shift):
    shift = shift % 128
    return pltpu.roll(x, shift, 1) if shift else x


class Du:
    def __init__(self, p, t):
        self.p, self.t = p, t

    def __add__(self, o):
        return Du(self.p + o.p, self.t + o.t)

    def __sub__(self, o):
        return Du(self.p - o.p, self.t - o.t)

    def __mul__(self, o):
        if isinstance(o, Du):
            return Du(self.p * o.p, self.p * o.t + self.t * o.p)
        return Du(self.p * o, self.t * o)


def primitive(u):
    inv = 1.0 / u[0].p

    def over_density(x):
        value = x.p * inv
        return Du(value, (x.t - value * u[0].t) * inv)

    vel = [over_density(u[i]) for i in (1, 2, 3)]
    kinetic = (u[1] * vel[0] + u[2] * vel[1] + u[3] * vel[2]) * 0.5
    pressure = (u[4] - kinetic) * (GAMMA - 1.0)
    return vel, pressure, over_density(pressure)


def wave_square(vel, temper):
    return vel[0] * vel[0] + vel[1] * vel[1] + vel[2] * vel[2] + temper * GAMMA


def viscous(vel, q, a):
    div = q[0][0] + q[1][1] + q[2][2]
    stress = []
    for b in range(3):
        s = q[a][b] + q[b][a]
        if b == a:
            s = s - div * (2.0 / 3.0)
        stress.append(s * VISC)
    energy = stress[0] * vel[0] + stress[1] * vel[1] + stress[2] * vel[2] + q[a][3] * COND
    return stress + [energy]


def block(start):
    return pl.ds(pl.multiple_of(start, 8), 8)


def lanes(width=128):
    return lax.broadcasted_iota(jnp.int32, (8, width), 1)


def parity(axis):
    return lax.rem(lax.axis_index(axis), 2) == 0


def own_keys(width):
    j = lax.broadcasted_iota(jnp.int32, (1, width), 1)
    g = (j >= C).astype(jnp.int32) + (j >= 2 * C).astype(jnp.int32) + (j >= 3 * C).astype(jnp.int32)
    return (4 * (j - C * g) + g).astype(F32)


def column(row):
    shape = (C, row.shape[1])
    diagonal = lax.broadcasted_iota(jnp.int32, shape, 0) == lax.broadcasted_iota(jnp.int32, shape, 1)
    return jnp.sum(jnp.where(diagonal, row, 0.0), axis=1, keepdims=True)


def tile_of(pt, l):
    return slice((pt * L + l) * 128, (pt * L + l + 1) * 128)


def send_parts(send_ref, tab_ref, be_ref, bo_ref, ze_ref, zo_ref, terms):
    even = parity("stream")
    low = send_ref[0, 0:1, :].astype(F32)
    up = send_ref[0, 1:2, :].astype(F32)
    keys = own_keys(4 * C)
    ones = [
        (column(jnp.where(even, x, y)) == keys).astype(BF16) for x, y in ((up, low), (low, up))
    ]
    sent = choose(jnp.concatenate(ones, axis=0), tab_ref[: 4 * C, :], terms)
    be_ref[...] = sent[:SLOTS]
    bo_ref[...] = sent[C : C + SLOTS]
    even_z = parity("span")
    for pt in range(2):
        bottom = tab_ref[4 * C : 5 * C, tile_of(pt, 0)]
        top = tab_ref[5 * C : 6 * C, tile_of(pt, L - 1)]
        cols = slice(pt * 128, (pt + 1) * 128)
        ze_ref[:, cols] = jnp.where(even_z, top, bottom)
        zo_ref[:, cols] = jnp.where(even_z, bottom, top)


def join_received(rcv, re_ref, ro_ref):
    rcv[...] = jnp.zeros(rcv.shape, F32)
    rcv[:SLOTS, :] = re_ref[...]
    rcv[C : C + SLOTS, :] = ro_ref[...]


def spanwise(tab_ref, rze_ref, rzo_ref, even_z, rows, pt, l):
    cols = slice(pt * 128, (pt + 1) * 128)
    if l == 0:
        lower = jnp.where(even_z, rzo_ref[block(rows), cols], rze_ref[block(rows), cols])
        return lower, tab_ref[block(4 * C + rows), tile_of(pt, 1)]
    upper = jnp.where(even_z, rze_ref[block(rows), cols], rzo_ref[block(rows), cols])
    return tab_ref[block(5 * C + rows), tile_of(pt, 0)], upper


def traces_kernel(state_hbm, dir_hbm, trace_hbm, send_ref, xs, tab_ref, be_ref, bo_ref, ze_ref, zo_ref, sbuf, dbuf, tbuf, sems):
    copies = [
        pltpu.make_async_copy(src, dst, sems.at[i])
        for i, (src, dst) in enumerate(((state_hbm, sbuf), (dir_hbm, dbuf), (trace_hbm, tbuf)))
    ]
    for copy in copies:
        copy.start()
    xs[:, 512:640] = jnp.zeros((2 * R, 128), F32)
    for pt, ref in enumerate((sbuf, dbuf)):
        copies[pt].wait()
        for l in range(L):
            xs[pt * R + l * C : pt * R + (l + 1) * C, 0:625] = ref[:, l, :]
    copies[2].wait()
    for i in range(3):
        faces = pick(xs[...], tbuf[:, i * 256 : (i + 1) * 256])
        for side in range(2):
            for pt in range(2):
                for l in range(L):
                    at = pt * R + l * C
                    tab_ref[(2 * i + side) * C : (2 * i + side + 1) * C, tile_of(pt, l)] = faces[at : at + C, side * 128 : (side + 1) * 128]
    send_parts(send_ref, tab_ref, be_ref, bo_ref, ze_ref, zo_ref, 3)


def load(ref, count, rows, cols):
    return [Du(ref[block(v * R + rows), cols], ref[block((count + v) * R + rows), cols]) for v in range(count)]


def store(ref, count, v, rows, cols, value):
    ref[block(v * R + rows), cols] = value.p
    ref[block((count + v) * R + rows), cols] = value.t


ALL = slice(None)


def before_kernel(xs, tab_ref, metric_ref, fs_ref, sel_ref, grad_ref, u_ref, fl_ref, w_ref, q_ref, m_ref, ones_ref, wall_ref, own_ref):
    lane = lanes()
    for pt in range(2):

        def body(rb, carry):
            tiles = [xs[block(pt * R + rb * 8), t * 128 : (t + 1) * 128] for t in range(5)]
            for v in range(5):
                value = roll(tiles[v], 3 * v)
                if v:
                    value = jnp.where(lane < 3 * v, roll(tiles[v - 1], 3 * v), value)
                pad = 1.0 if pt == 0 and v in (0, 4) else 0.0
                u_ref[block((pt * 5 + v) * R + rb * 8), :] = jnp.where(lane < 125, value, pad)
            return carry

        lax.fori_loop(0, R // 8, body, 0)
    for l in range(L):
        for a in range(3):
            m_ref[l * C : (l + 1) * C, a : a + 1] = column(metric_ref[a, l : l + 1, :])
    even = parity("stream")
    keys = own_keys(4 * C)
    j = lax.broadcasted_iota(jnp.int32, (1, 2 * C), 1)
    near = jnp.where(j < C, j, j - C)
    named = 4 * C + near + jnp.where((j < C) == even, SLOTS, 0)
    far = jnp.where(near < SLOTS, named, -5).astype(F32)
    at = lax.broadcasted_iota(jnp.int32, (C, 1), 0).astype(F32) * 4.0
    for f in range(4):
        col = column(fs_ref[f : f + 1, :].astype(F32))
        wall = col < 0.0
        col = jnp.where(wall, at + float(f), col)
        ones_ref[f * C : (f + 1) * C, 0 : 4 * C] = (col == keys).astype(BF16)
        ones_ref[f * C : (f + 1) * C, 256 : 256 + 2 * C] = (col == far).astype(BF16)
        wall_ref[f * C : (f + 1) * C, :] = jnp.broadcast_to(jnp.where(wall, -1.0, 1.0), (C, 128))
    own_ref[...] = choose(ones_ref[:, : 4 * C], tab_ref[: 4 * C, :])

    def fields(rb, carry):
        rows = rb * 8
        vel, _, temper = primitive(load(u_ref, 5, rows, ALL))
        for f, value in enumerate(vel + [temper]):
            store(w_ref, 4, f, rows, ALL, value)
        return carry

    lax.fori_loop(0, R // 8, fields, 0)
    q_ref[...] = mm3(w_ref[...], grad_ref[:128, :], grad_ref[128:, :])
    fl_ref[...] = pick(u_ref[...], sel_ref[...])


def gradient_kernel(
    send_ref, tab_ref, w_ref, q_ref, m_ref, ones_ref, wall_ref, own_ref, re_ref, ro_ref, rze_ref, rzo_ref,
    lxy_ref, lz_ref, tv_ref,
    out_ref, vv, vtab_ref, be_ref, bo_ref, ze_ref, zo_ref,
    rcv, got, wo, ql,
):
    join_received(rcv, re_ref, ro_ref)
    got[...] = own_ref[...] + choose(ones_ref[:, 256 : 256 + 2 * C], rcv[...])
    even_z = parity("span")
    lane = lanes()
    moment = (lane >= 25) & (lane < 100)

    def outside(cb, carry):
        rows = cb * 8
        flip = [None, None] + [jnp.where(moment, wall_ref[block(f * C + rows), :], 1.0) for f in (2, 3)]
        for l in range(L):
            state = []
            for pt in range(2):
                picked = [got[block(f * C + rows), tile_of(pt, l)] for f in range(4)]
                picked = [x if s is None else x * s for x, s in zip(picked, flip)]
                lower, upper = spanwise(tab_ref, rze_ref, rzo_ref, even_z, rows, pt, l)
                both = []
                for v in range(5):
                    at = block((pt * 5 + v) * R + l * C + rows)
                    pad = 1.0 if pt == 0 and v in (0, 4) else 0.0
                    acc = roll(picked[0], -25 * v)
                    for f in range(1, 4):
                        acc = jnp.where(lane >= 25 * f, roll(picked[f], 25 * (f - v)), acc)
                    acc = jnp.where(lane >= 100, pad, acc)
                    edge = jnp.where(lane < 25, roll(lower, -25 * v), jnp.where(lane < 50, roll(upper, 25 - 25 * v), pad))
                    out_ref[at, :128] = acc
                    out_ref[at, 128:] = edge
                    both.append((acc, edge))
                state.append(both)
            for half in range(2):
                u = [Du(state[0][v][half], state[1][v][half]) for v in range(5)]
                vel, _, temper = primitive(u)
                for f, value in enumerate(vel + [temper]):
                    store(wo, 4, f, l * C + rows, slice(half * 128, (half + 1) * 128), value)
        return carry

    lax.fori_loop(0, C // 8, outside, 0)
    ql[:, :256] = pick(wo[:, :128], lxy_ref[...], 2)
    ql[:, 256:] = pick(wo[:, 128:], lz_ref[...], 2)

    def stresses(rb, carry):
        rows = rb * 8
        vel = [Du(w_ref[block(f * R + rows), :], w_ref[block((4 + f) * R + rows), :]) for f in range(3)]
        q = []
        for a in range(3):
            scale = m_ref[block(rows), a : a + 1]
            cols = slice(a * 128, (a + 1) * 128)
            q.append([(x + y) * scale for x, y in zip(load(q_ref, 4, rows, cols), load(ql, 4, rows, cols))])
        for a in range(3):
            for v, value in enumerate(viscous(vel, q, a)):
                cols = slice((a * 4 + v) * 128, (a * 4 + v + 1) * 128)
                vv[block(rows), cols] = value.p
                vv[block(R + rows), cols] = value.t
        return carry

    lax.fori_loop(0, R // 8, stresses, 0)
    for a in range(3):
        faces = pick(vv[:, a * 512 : (a + 1) * 512], tv_ref[a * 512 : (a + 1) * 512, :], 2)
        for side in range(2):
            for pt in range(2):
                for l in range(L):
                    at = pt * R + l * C
                    vtab_ref[(2 * a + side) * C : (2 * a + side + 1) * C, tile_of(pt, l)] = faces[at : at + C, side * 128 : (side + 1) * 128]
    send_parts(send_ref, vtab_ref, be_ref, bo_ref, ze_ref, zo_ref, 2)


def inner_kernel(u_ref, fl_ref, out_ref, vv_ref, vtab_ref, ones_ref, m_ref, sg_ref, div_ref, sc_ref, part_ref, own_ref, fv, surf_ref):
    lane = lanes(256)
    own_ref[...] = choose(ones_ref[:, : 4 * C], vtab_ref[: 4 * C, :], 2)

    def volume(rb, carry):
        rows = rb * 8
        u = load(u_ref, 5, rows, ALL)
        vel, pressure, _ = primitive(u)
        total = u[4] + pressure
        for a in range(3):
            cols = slice(a * 128, (a + 1) * 128)
            scale = m_ref[block(rows), a : a + 1]
            visc = []
            for v in range(4):
                at = slice((a * 4 + v) * 128, (a * 4 + v + 1) * 128)
                visc.append(Du(vv_ref[block(rows), at], vv_ref[block(R + rows), at]))
            store(fv, 5, 0, rows, cols, u[1 + a] * scale)
            for i in range(3):
                flux = u[1 + i] * vel[a]
                if i == a:
                    flux = flux + pressure
                store(fv, 5, 1 + i, rows, cols, (flux - visc[i]) * scale)
            store(fv, 5, 4, rows, cols, (total * vel[a] - visc[3]) * scale)
        return carry

    lax.fori_loop(0, R // 8, volume, 0)

    def by_lane(x, y, z):
        return jnp.where(lane < 50, x, jnp.where(lane < 128, y, z))

    def normal(vals):
        return Du(by_lane(*[d.p for d in vals]), by_lane(*[d.t for d in vals]))

    def surface(rb, carry):
        rows = rb * 8
        inner = load(fl_ref, 5, rows, ALL)
        vel, _, temper = primitive(inner)
        speed2 = wave_square(vel, temper)
        outer = load(out_ref, 5, rows, ALL)
        vel, pressure, temper = primitive(outer)
        speed2 = (speed2 + wave_square(vel, temper)) * 0.5
        root = jnp.sqrt(speed2.p)
        speed = Du(root, 0.5 * speed2.t / root)
        mface = by_lane(*[m_ref[block(rows), a : a + 1] for a in range(3)])
        lift_s = sg_ref[0:1, :] * mface
        speed = speed * (sg_ref[1:2, :] * mface)
        vn = normal(vel)
        fluxes = [normal(outer[1:4])]
        for i in range(3):
            flux = outer[1 + i] * vn
            side = (lane < 50) if i == 0 else ((lane >= 50) & (lane < 128)) if i == 1 else (lane >= 128)
            fluxes.append(Du(flux.p + jnp.where(side, pressure.p, 0.0), flux.t + jnp.where(side, pressure.t, 0.0)))
        fluxes.append((outer[4] + pressure) * vn)
        for v in range(5):
            store(surf_ref, 5, v, rows, ALL, fluxes[v] * lift_s - speed * (outer[v] - inner[v]))
        return carry

    lax.fori_loop(0, R // 8, surface, 0)
    part_ref[...] = mm3(fv[...], div_ref[:384, :], div_ref[384:, :]) + pick(surf_ref[...], sc_ref[...], 2)


def unpack(tiles, lane, t):
    value = roll(tiles[t], -3 * t)
    if t < 4:
        value = jnp.where(lane < 125 - 3 * t, value, roll(tiles[t + 1], -3 * (t + 1)))
    return value


def final_kernel(
    vtab_ref, ones_ref, own_ref, re_ref, ro_ref, rze_ref, rzo_ref, m_ref, part_ref, u_ref, pv_ref,
    res_ref, prod_ref, sums_ref,
    rcv, got, vx, vo, xs,
):
    join_received(rcv, re_ref, ro_ref)
    got[...] = own_ref[...] + choose(ones_ref[:, 256 : 256 + 2 * C], rcv[...], 2)
    even_z = parity("span")

    def gather(cb, carry):
        rows = cb * 8
        for l in range(L):
            scale = [m_ref[block(l * C + rows), a : a + 1] * HALF_LIFT for a in range(3)]
            for pt in range(2):
                at = block(pt * R + l * C + rows)
                values = [got[block(f * C + rows), tile_of(pt, l)] for f in range(4)]
                values += list(spanwise(vtab_ref, rze_ref, rzo_ref, even_z, rows, pt, l))
                for f, value in enumerate(values):
                    value = value * scale[f // 2]
                    vx[at, f * 128 : (f + 1) * 128] = value if f % 2 == 0 else -value
        return carry

    lax.fori_loop(0, C // 8, gather, 0)
    vo[...] = pick(vx[...], pv_ref[...], 2)
    lane = lanes()

    def output(rb, sums):
        sums = list(sums)
        rows = rb * 8
        prod = []
        for pt in range(2):
            tiles = [part_ref[block((pt * 5 + v) * R + rows), :] for v in range(5)]
            for v in range(4):
                tiles[v + 1] = tiles[v + 1] + vo[block(pt * R + rows), v * 128 : (v + 1) * 128]
            tiles = [jnp.where(lane < 125, x, 0.0) for x in tiles]
            for t in range(5):
                xs[block(pt * R + rows), t * 128 : (t + 1) * 128] = unpack(tiles, lane, t)
            prod.append(tiles)
        for v in range(5):
            d = u_ref[block((5 + v) * R + rows), :]
            res, p = prod[0][v], prod[1][v]
            for i, x in enumerate((d * p, d * d, res * res, p * p)):
                sums[i] = sums[i] + x
        return tuple(sums)

    zero = jnp.zeros((8, 128), F32)
    sums = lax.fori_loop(0, R // 8, output, (zero, zero, zero, zero))
    lane1 = lax.broadcasted_iota(jnp.int32, (1, 128), 1)
    row = jnp.zeros((1, 128), F32)
    for i, x in enumerate(sums):
        x = jnp.sum(jnp.sum(x, axis=0, keepdims=True), axis=1, keepdims=True)
        row = jnp.where(lane1 == i, x, row)
    sums_ref[...] = row
    for pt, ref in enumerate((res_ref, prod_ref)):
        for l in range(L):
            ref[:, l, :] = xs[pt * R + l * C : pt * R + (l + 1) * C, 0:625]


def scale_kernel(all_ref, prod_ref, dir_ref, basis_ref, krylov_ref, *, total):
    sums = jnp.sum(all_ref[...], axis=0, keepdims=True)
    dp, dd, rr, pp = [sums[:, i : i + 1] for i in range(4)]
    coefficient = dp / total
    beta = jnp.sqrt((pp - 2.0 * coefficient * dp + coefficient * coefficient * dd) / total)
    norm = jnp.sqrt(rr / total)
    for i, x in enumerate((coefficient, beta, norm)):
        krylov_ref[i] = x[0, 0]
    basis_ref[...] = (prod_ref[...] - coefficient.reshape(1, 1, 1) * dir_ref[...]) / beta.reshape(1, 1, 1)


def shaped(*dims):
    return jax.ShapeDtypeStruct(dims, F32)


def vmem(*dims):
    return pltpu.VMEM(dims, F32)


def pairs_of(count):
    first = [(i, i ^ 1) for i in range(count)]
    second = [(i, (((i + 1) ^ 1) - 1) % count) for i in range(count)]
    return first, second


def exchange(be, bo, ze, zo):
    se, so = pairs_of(lax.axis_size("stream"))
    pe, po = pairs_of(lax.axis_size("span"))
    return (
        lax.ppermute(be, "stream", se),
        lax.ppermute(bo, "stream", so),
        lax.ppermute(ze, "span", pe),
        lax.ppermute(zo, "span", po),
    )


SENT = (shaped(SLOTS, 512), shaped(SLOTS, 512), shaped(C, 256), shaped(C, 256))
VMEM_LIMIT = 20 * 2**20


def call(kernel, name, out_shape, scratch=(), **kwargs):
    params = pltpu.CompilerParams(vmem_limit_bytes=VMEM_LIMIT)
    return pl.pallas_call(kernel, out_shape=out_shape, scratch_shapes=list(scratch), name=name, compiler_params=params, **kwargs)


def local(state, direction, metric, face_source, send_rows):
    hbm = pl.BlockSpec(memory_space=pltpu.HBM)
    whole = pl.BlockSpec(memory_space=pltpu.VMEM)
    xs, tab, *sent = call(
        traces_kernel,
        "traces",
        (shaped(2 * R, 640), shaped(6 * C, 512)) + SENT,
        (vmem(C, L, 625), vmem(C, L, 625), pltpu.VMEM((640, 768), BF16), pltpu.SemaphoreType.DMA((3,))),
        in_specs=[hbm, hbm, hbm, whole],
    )(state, direction, CONST["trace"], send_rows)
    got = exchange(*sent)
    u, fl, w, q, m, ones, wall, own = call(
        before_kernel,
        "before",
        (
            shaped(10 * R, 128), shaped(10 * R, 256), shaped(8 * R, 128), shaped(8 * R, 384), shaped(R, 128),
            jax.ShapeDtypeStruct((4 * C, 384), BF16), shaped(4 * C, 128), shaped(4 * C, 512),
        ),
    )(xs, tab, jnp.transpose(metric, (2, 1, 0)), face_source.T, CONST["sel"], CONST["grad"])
    out, vv, vtab, *sent = call(
        gradient_kernel,
        "gradient",
        (shaped(10 * R, 256), shaped(2 * R, 1536), shaped(6 * C, 512)) + SENT,
        (vmem(2 * C, 512), vmem(4 * C, 512), vmem(8 * R, 256), vmem(8 * R, 384)),
    )(send_rows, tab, w, q, m, ones, wall, own, *got, CONST["lift_xy"], CONST["lift_z"], CONST["trace_v"])
    got = exchange(*sent)
    part, own = call(
        inner_kernel,
        "inner",
        (shaped(10 * R, 128), shaped(4 * C, 512)),
        (vmem(10 * R, 384), vmem(10 * R, 256)),
    )(u, fl, out, vv, vtab, ones, m, CONST["signs"], CONST["div"], CONST["scatter"])
    residual, product, sums = call(
        final_kernel,
        "final",
        (shaped(C, L, 625), shaped(C, L, 625), shaped(1, 128)),
        (vmem(2 * C, 512), vmem(4 * C, 512), vmem(2 * R, 768), vmem(2 * R, 512), vmem(2 * R, 640)),
    )(vtab, ones, own, *got, m, part, u, CONST["place_v"])
    axes = ("stream", "span")
    count = lax.axis_size("stream") * lax.axis_size("span")
    spread = jnp.broadcast_to(sums[None], (count, 1, 128))
    everyone = lax.all_to_all(spread, axes, 0, 0, tiled=True).reshape(count, 128)
    total = float(state.size * count)
    basis, krylov = call(
        lambda *refs: scale_kernel(*refs, total=total),
        "scale",
        (shaped(C, L, 625), shaped(3)),
        out_specs=(whole, pl.BlockSpec(memory_space=pltpu.SMEM)),
    )(everyone, product, direction)
    return residual, basis, krylov


def solution(mesh):
    cells = P("stream", "span", None)
    in_specs = (cells, cells, cells, P("stream", None), P("stream", None, None))
    out_specs = (cells, cells, P())
    return jax.shard_map(local, mesh=mesh, in_specs=in_specs, out_specs=out_specs, check_vma=False)
```

time: 77.3 us -> 61.8 us (0.80)
  Pallas kernels: 27.2 us -> 14.4 us
  waiting for transfers between devices: 1.78 us -> 0.02 us
  local copies, waits for them, and re-layouts: 5.25 us -> 3.87 us
  blocking collectives: 20.3 us -> 21.3 us
    pallas_call x5 -> x6, Pallas kernels: 27.2 us -> 14.4 us  [the longest x1 3.17 us: local(): call(gradient_kernel, 'gradient', (shaped(10 * R, 256), shaped(2 * R, 153...]
    ppermute x2, waiting for transfers between devices: 1.76 us -> 0.01 us  [exchange(): lax.ppermute(zo, 'span', po)]
    all_to_all x1, blocking collectives: 20.3 us -> 21.3 us  [local(): lax.all_to_all(spread, axes, 0, 0, tiled=True).reshape(count, 128)]
    unnamed x24 -> x32, local copies, waits for them, and re-layouts: 4.67 us -> 3.8 us
  transfers between devices with their start and end apart: 8 -> 8, of which waited for: 1 -> 0; matrix products, arithmetic and copies ran while one was open for 1% -> 0% of each run, Pallas kernels for 7% -> 9%
where the time goes in v1:
time: 61.8 us; the launch traced here: 61.6 us
  blocking collectives  21.3 us (34%)
  starting transfers between devices  21.1 us (34%)
  Pallas kernels  14.4 us (23%)
  local copies, waits for them, and re-layouts  3.87 us (6%)
  between operations  0.84 us (1%)
    all_to_all x1, blocking collectives, local(): lax.all_to_all(spread, axes, 0, 0, tiled=True).reshape(count, 128)  21.3 us
    ppermute x2, starting transfers between devices, exchange(): lax.ppermute(bo, 'stream', so)  11.3 us
    ppermute x2, starting transfers between devices, exchange(): lax.ppermute(be, 'stream', se)  3.91 us
    unnamed x32, local copies, waits for them, and re-layouts  3.8 us
    ppermute x2, starting transfers between devices, exchange(): lax.ppermute(ze, 'span', pe)  3.53 us
    pallas_call x1, Pallas kernels, local(): call(gradient_kernel, 'gradient', (shaped(10 * R, 256), shaped(2 * R, 153...  3.17 us
    pallas_call x1, Pallas kernels, local(): call(before_kernel, 'before', (shaped(10 * R, 128), shaped(10 * R, 256),...  2.9 us
    pallas_call x1, Pallas kernels, local(): call(inner_kernel, 'inner', (shaped(10 * R, 128), shaped(4 * C, 512)), (v...  2.84 us
  transfers between devices with their start and end apart: 8, of which 0 were waited for; matrix products, arithmetic and copies ran while one was open for 0% of the time, Pallas kernels for 9%

profile of v1, /device:TPU:1, one launch (start us, length us, event | category | flops | bytes accessed | tf_op | source)
XLA Modules:
  0.0 61.6 jit_solution(2671476832940304041)
XLA Ops:
  0.6 0.0 copy-start
  0.6 1.2 %copy-done = bf16[640,768]{1,0:T(8,128)(2,1)S(1)} copy-done((bf16[640,768]{1,0:T(8,128)(2,1)S(1)}, bf16[640,768]{1,0:T(8,128)(2,1)}, u32[]{:S(2)}) %copy-start) | copy-done | bytes 983064
  1.8 0.0 copy-start.1
  1.8 0.9 %copy-done.1 = f32[40,2,625]{2,1,0:T(2,128)S(1)} copy-done((f32[40,2,625]{2,1,0:T(2,128)S(1)}, f32[40,2,625]{2,1,0:T(2,128)}, u32[]{:S(2)}) %copy-start.1) | copy-done | bytes 200024
  2.8 0.0 copy-start.5
  2.8 0.9 %copy-done.5 = f32[40,2,625]{2,1,0:T(2,128)S(1)} copy-done((f32[40,2,625]{2,1,0:T(2,128)S(1)}, f32[40,2,625]{2,1,0:T(2,128)}, u32[]{:S(2)}) %copy-start.5) | copy-done | bytes 200024
  3.7 0.0 copy-start.13
  3.7 0.7 %copy-done.13 = s32[1,2,33]{2,1,0:T(2,128)S(1)} copy-done((s32[1,2,33]{2,1,0:T(2,128)S(1)}, s32[1,2,33]{2,1,0:T(2,128)}, u32[]{:S(2)}) %copy-start.13) | copy-done | bytes 288
  4.4 0.0 copy-start.6
  4.4 0.0 copy-start.10
  4.4 0.0 copy-start.14
  4.4 0.0 copy-start.15
  4.4 1.9 %traces.1 = (f32[160,640]{1,0:T(8,128)S(1)}, f32[240,512]{1,0:T(8,128)S(1)}, f32[33,512]{1,0:T(8,128)S(1)}, f32[33,512]{1,0:T(8,128)S(1)}, f32[40,256]{1,0:T(8,128)S(1)}, /*index=5*/f32[40,256]{1,0:T(8,128)S(1)}) custom-call(f32[40,2,625]{2,1,0:T(2,128)S(1)} %copy-done.5, f32[40,2,625]{2,1,0:T(2,128)S(1)} %copy-done.1, bf16[640,768]{1,0:T(8,128)(2,1)S(1)} %copy-done, ...), custom_call_target="tpu_custom_call" | custom-call | tf_op jit(solution)/shard_map/traces/pallas_call | solution.py:572
  6.3 0.0 copy-start.4
  6.3 3.8 %collective-permute-start = (f32[33,512]{1,0:T(8,128)S(1)}, f32[33,512]{1,0:T(8,128)S(1)}, u32[]{:S(2)}, u32[]{:S(2)}) collective-permute-start(f32[33,512]{1,0:T(8,128)S(1)} %get-tuple-element.39), channel_id=1, source_target_pairs={{0,4},{4,0},{8,12},{12,8},{16,20},{20,16},{24,28},{28,24},{32,36},... | collective-permute-start | bytes 202760 | tf_op jit(solution)/shard_map/ppermute | solution.py:553
  10.1 7.6 %collective-permute-start.1 = (f32[33,512]{1,0:T(8,128)S(1)}, f32[33,512]{1,0:T(8,128)S(1)}, u32[]{:S(2)}, u32[]{:S(2)}) collective-permute-start(f32[33,512]{1,0:T(8,128)S(1)} %get-tuple-element.40), channel_id=1, source_target_pairs={{0,252},{4,8},{8,4},{12,16},{16,12},{20,24},{24,20},{28,32},{32,28... | collective-permute-start | bytes 202760 | tf_op jit(solution)/shard_map/ppermute | solution.py:554
  17.7 1.2 %collective-permute-start.2 = (f32[40,256]{1,0:T(8,128)S(1)}, f32[40,256]{1,0:T(8,128)S(1)}, u32[]{:S(2)}, u32[]{:S(2)}) collective-permute-start(f32[40,256]{1,0:T(8,128)S(1)} %get-tuple-element.41), channel_id=1, source_target_pairs={{0,1},{1,0},{2,3},{3,2},{4,5},{5,4},{6,7},{7,6},{8,9},{9,8},{10,11... | collective-permute-start | bytes 122888 | tf_op jit(solution)/shard_map/ppermute | solution.py:555
  18.9 1.2 %collective-permute-start.3 = (f32[40,256]{1,0:T(8,128)S(1)}, f32[40,256]{1,0:T(8,128)S(1)}, u32[]{:S(2)}, u32[]{:S(2)}) collective-permute-start(f32[40,256]{1,0:T(8,128)S(1)} %get-tuple-element.42), channel_id=1, source_target_pairs={{0,3},{1,2},{2,1},{3,0},{4,7},{5,6},{6,5},{7,4},{8,11},{9,10},{10,... | collective-permute-start | bytes 122888 | tf_op jit(solution)/shard_map/ppermute | solution.py:556
  20.1 0.0 copy-done.6
  20.1 0.0 copy-done.10
  20.1 0.0 copy-done.14
  20.1 0.0 copy-done.15
  20.1 0.0 copy-start.9
  20.1 0.0 copy-start.11
  20.1 2.9 %before.1 = (f32[800,128]{1,0:T(8,128)S(1)}, f32[800,256]{1,0:T(8,128)S(1)}, f32[640,128]{1,0:T(8,128)S(1)}, f32[640,384]{1,0:T(8,128)S(1)}, f32[80,128]{1,0:T(8...) custom-call(f32[160,640]{1,0:T(8,128)S(1)} %get-tuple-element.32.xs, ...), custom_call_target="tpu_custom_call" | custom-call | tf_op jit(solution)/shard_map/before/pallas_call | solution.py:580
  23.0 0.0 collective-permute-done.2.rze_ref
  23.0 0.0 collective-permute-done.3.rzo_ref
  23.1 0.0 collective-permute-done.re_ref
  23.1 0.0 collective-permute-done.1.ro_ref
  23.1 0.0 copy-done.4
  23.1 0.0 copy-done.9
  23.1 0.0 copy-done.11
  23.1 0.0 copy-start.7
  23.1 0.0 copy-start.8
  23.1 3.2 %gradient.1 = (f32[800,256]{1,0:T(8,128)S(1)}, f32[160,1536]{1,0:T(8,128)S(1)}, f32[240,512]{1,0:T(8,128)S(1)}, f32[33,512]{1,0:T(8,128)S(1)}, f32[33,512]{1,0:T...) custom-call(s32[1,2,33]{2,1,0:T(2,128)S(1)} %copy-done.13, f32[240,512]{1,0:T(8,128)S(1)} %get-tuple-element.31.tab_ref, ...), custom_call_target="tpu_custom_call" | custom-call | tf_op jit(solution)/shard_map/gradient/pallas_call | solution.py:588
  26.3 0.0 copy-start.12
  26.3 0.1 collective-permute-start.4
  26.4 3.7 %collective-permute-start.5 = (f32[33,512]{1,0:T(8,128)S(1)}, f32[33,512]{1,0:T(8,128)S(1)}, u32[]{:S(2)}, u32[]{:S(2)}) collective-permute-start(f32[33,512]{1,0:T(8,128)S(1)} %get-tuple-element.50), channel_id=1, source_target_pairs={{0,252},{4,8},{8,4},{12,16},{16,12},{20,24},{24,20},{28,32},{32,28... | collective-permute-start | bytes 202760 | tf_op jit(solution)/shard_map/ppermute | solution.py:554
  30.1 2.3 %collective-permute-start.6 = (f32[40,256]{1,0:T(8,128)S(1)}, f32[40,256]{1,0:T(8,128)S(1)}, u32[]{:S(2)}, u32[]{:S(2)}) collective-permute-start(f32[40,256]{1,0:T(8,128)S(1)} %get-tuple-element.51), channel_id=1, source_target_pairs={{0,1},{1,0},{2,3},{3,2},{4,5},{5,4},{6,7},{7,6},{8,9},{9,8},{10,11... | collective-permute-start | bytes 122888 | tf_op jit(solution)/shard_map/ppermute | solution.py:555
  32.5 1.2 %collective-permute-start.7 = (f32[40,256]{1,0:T(8,128)S(1)}, f32[40,256]{1,0:T(8,128)S(1)}, u32[]{:S(2)}, u32[]{:S(2)}) collective-permute-start(f32[40,256]{1,0:T(8,128)S(1)} %get-tuple-element.52), channel_id=1, source_target_pairs={{0,3},{1,2},{2,1},{3,0},{4,7},{5,6},{6,5},{7,4},{8,11},{9,10},{10,... | collective-permute-start | bytes 122888 | tf_op jit(solution)/shard_map/ppermute | solution.py:556
  33.7 0.0 copy-done.7
  33.7 0.0 copy-done.8
  33.7 0.0 copy-done.12
  33.7 0.0 copy-start.3
  33.7 2.8 %inner.1 = (f32[800,128]{1,0:T(8,128)S(1)}, f32[160,512]{1,0:T(8,128)S(1)}) custom-call(f32[800,128]{1,0:T(8,128)S(1)} %get-tuple-element.44.u_ref, f32[800,256]{1,0:T(8,128)S(1)} %get-tuple-element.45.fl_ref, f32[800,256]{1,0:T(8,128)S(1)} %get-tuple-element.46.out_ref, f32[160,1536]{1,0:T(8,128)S(1)} %get-tuple-element.47.vv_ref, ...), custom_call_target="tpu_custom_call" | custom-call | tf_op jit(solution)/shard_map/inner/pallas_call | solution.py:595
  36.5 0.0 collective-permute-done.6.rze_ref
  36.5 0.0 collective-permute-done.7.rzo_ref
  36.5 0.0 collective-permute-done.4.re_ref
  36.6 0.0 collective-permute-done.5.ro_ref
  36.6 0.0 copy-done.3
  36.6 2.6 %final.1 = (f32[40,2,625]{2,1,0:T(2,128)}, f32[40,2,625]{2,1,0:T(2,128)S(1)}, f32[1,128]{1,0:T(1,128)S(1)}) custom-call(f32[240,512]{1,0:T(8,128)S(1)} %get-tuple-element.43.vtab_ref, bf16[160,384]{1,0:T(8,128)(2,1)S(1)} %get-tuple-element.36.ones_ref, f32[160,512]{1,0:T(8,128)S(1)} %get-tuple-element.48.own_ref, ...), custom_call_target="tpu_custom_call" | custom-call | tf_op jit(solution)/shard_map/final/pallas_call | solution.py:601
  39.2 0.0 copy-start.2
  39.2 0.1 broadcast_in_dim.9
  39.2 21.3 %all_to_all.5 = f32[256,1,128]{2,1,0:T(1,128)S(1)} all-to-all(f32[256,1,128]{2,1,0:T(1,128)S(1)} %broadcast_in_dim.9), channel_id=1, replica_groups=mesh['stream'=64,'span'=4] {'stream','span'}, dimensions={0} | all-to-all | bytes 262144 | tf_op jit(solution)/shard_map/all_to_all | solution.py:610
  60.6 0.0 copy-done.2
  60.6 1.0 %scale.1 = (f32[40,2,625]{2,1,0:T(2,128)}, f32[3]{0:T(128)}) custom-call(f32[256,128]{1,0:T(8,128)S(1)} %bitcast.4, f32[40,2,625]{2,1,0:T(2,128)S(1)} %get-tuple-element.56.refs_1_, f32[40,2,625]{2,1,0:T(2,128)S(1)} %copy-done.2), custom_call_target="tpu_custom_call" | custom-call | tf_op jit(solution)/shard_map/scale/pallas_call | solution.py:612
Async XLA Ops:
  0.6 1.2 %copy-start = (bf16[640,768]{1,0:T(8,128)(2,1)S(1)}, bf16[640,768]{1,0:T(8,128)(2,1)}, u32[]{:S(2)}) copy-start(bf16[640,768]{1,0:T(8,128)(2,1)} %constant.20.clone.trace_hbm) | copy-start | bytes 2949124
  1.8 0.9 %copy-start.1 = (f32[40,2,625]{2,1,0:T(2,128)S(1)}, f32[40,2,625]{2,1,0:T(2,128)}, u32[]{:S(2)}) copy-start(f32[40,2,625]{2,1,0:T(2,128)} %refs_2_.1) | copy-start | bytes 600004
  2.8 0.9 %copy-start.5 = (f32[40,2,625]{2,1,0:T(2,128)S(1)}, f32[40,2,625]{2,1,0:T(2,128)}, u32[]{:S(2)}) copy-start(f32[40,2,625]{2,1,0:T(2,128)} %state_hbm.1) | copy-start | bytes 600004
  3.7 0.7 %copy-start.13 = (s32[1,2,33]{2,1,0:T(2,128)S(1)}, s32[1,2,33]{2,1,0:T(2,128)}, u32[]{:S(2)}) copy-start(s32[1,2,33]{2,1,0:T(2,128)} %send_ref.3) | copy-start | bytes 796
  4.4 15.7 %copy-start.6 = (bf16[256,384]{1,0:T(8,128)(2,1)S(1)}, bf16[256,384]{1,0:T(8,128)(2,1)}, u32[]{:S(2)}) copy-start(bf16[256,384]{1,0:T(8,128)(2,1)} %constant.22.clone.grad_ref) | copy-start | bytes 589828
  4.4 15.7 %copy-start.10 = (bf16[128,256]{1,0:T(8,128)(2,1)S(1)}, bf16[128,256]{1,0:T(8,128)(2,1)}, u32[]{:S(2)}) copy-start(bf16[128,256]{1,0:T(8,128)(2,1)} %constant.21.clone.sel_ref) | copy-start | bytes 196612
  4.4 15.7 %copy-start.14 = (f32[40,2,3]{0,1,2:T(2,128)S(1)}, f32[40,2,3]{0,1,2:T(2,128)}, u32[]{:S(2)}) copy-start(f32[40,2,3]{0,1,2:T(2,128)} %param.17) | copy-start | bytes 2884
  4.4 15.7 %copy-start.15 = (s32[40,4]{0,1:T(4,128)S(1)}, s32[40,4]{0,1:T(4,128)}, u32[]{:S(2)}) copy-start(s32[40,4]{0,1:T(4,128)} %param.18) | copy-start | bytes 1924
  6.3 16.8 %copy-start.4 = (bf16[1536,256]{1,0:T(8,128)(2,1)S(1)}, bf16[1536,256]{1,0:T(8,128)(2,1)}, u32[]{:S(2)}) copy-start(bf16[1536,256]{1,0:T(8,128)(2,1)} %constant.25.clone.tv_ref) | copy-start | bytes 2359300
  6.3 16.8 %collective-permute-start = (f32[33,512]{1,0:T(8,128)S(1)}, f32[33,512]{1,0:T(8,128)S(1)}, u32[]{:S(2)}, u32[]{:S(2)}) collective-permute-start(f32[33,512]{1,0:T(8,128)S(1)} %get-tuple-element.39), channel_id=1, source_target_pairs={{0,4},{4,0},{8,12},{12,8},{16,20},{20,16},{24,28},{28,24},{32,36},... | collective-permute-start | bytes 202760 | tf_op jit(solution)/shard_map/ppermute | solution.py:553
  10.1 12.9 %collective-permute-start.1 = (f32[33,512]{1,0:T(8,128)S(1)}, f32[33,512]{1,0:T(8,128)S(1)}, u32[]{:S(2)}, u32[]{:S(2)}) collective-permute-start(f32[33,512]{1,0:T(8,128)S(1)} %get-tuple-element.40), channel_id=1, source_target_pairs={{0,252},{4,8},{8,4},{12,16},{16,12},{20,24},{24,20},{28,32},{32,28... | collective-permute-start | bytes 202760 | tf_op jit(solution)/shard_map/ppermute | solution.py:554
  17.7 5.3 %collective-permute-start.2 = (f32[40,256]{1,0:T(8,128)S(1)}, f32[40,256]{1,0:T(8,128)S(1)}, u32[]{:S(2)}, u32[]{:S(2)}) collective-permute-start(f32[40,256]{1,0:T(8,128)S(1)} %get-tuple-element.41), channel_id=1, source_target_pairs={{0,1},{1,0},{2,3},{3,2},{4,5},{5,4},{6,7},{7,6},{8,9},{9,8},{10,11... | collective-permute-start | bytes 122888 | tf_op jit(solution)/shard_map/ppermute | solution.py:555
  18.9 4.1 %collective-permute-start.3 = (f32[40,256]{1,0:T(8,128)S(1)}, f32[40,256]{1,0:T(8,128)S(1)}, u32[]{:S(2)}, u32[]{:S(2)}) collective-permute-start(f32[40,256]{1,0:T(8,128)S(1)} %get-tuple-element.42), channel_id=1, source_target_pairs={{0,3},{1,2},{2,1},{3,0},{4,7},{5,6},{6,5},{7,4},{8,11},{9,10},{10,... | collective-permute-start | bytes 122888 | tf_op jit(solution)/shard_map/ppermute | solution.py:556
  20.1 3.0 %copy-start.9 = (bf16[128,256]{1,0:T(8,128)(2,1)S(1)}, bf16[128,256]{1,0:T(8,128)(2,1)}, u32[]{:S(2)}) copy-start(bf16[128,256]{1,0:T(8,128)(2,1)} %constant.23.clone.lxy_ref) | copy-start | bytes 196612
  20.1 3.0 %copy-start.11 = (bf16[128,128]{1,0:T(8,128)(2,1)S(1)}, bf16[128,128]{1,0:T(8,128)(2,1)}, u32[]{:S(2)}) copy-start(bf16[128,128]{1,0:T(8,128)(2,1)} %constant.24.clone.lz_ref) | copy-start | bytes 98308
  23.1 10.6 %copy-start.7 = (bf16[768,128]{1,0:T(8,128)(2,1)S(1)}, bf16[768,128]{1,0:T(8,128)(2,1)}, u32[]{:S(2)}) copy-start(bf16[768,128]{1,0:T(8,128)(2,1)} %constant.27.clone.div_ref) | copy-start | bytes 589828
  23.1 10.5 %copy-start.8 = (bf16[256,128]{1,0:T(8,128)(2,1)S(1)}, bf16[256,128]{1,0:T(8,128)(2,1)}, u32[]{:S(2)}) copy-start(bf16[256,128]{1,0:T(8,128)(2,1)} %constant.28.clone.sc_ref) | copy-start | bytes 196612
  26.3 7.4 %copy-start.12 = (f32[8,256]{1,0:T(8,128)S(1)}, f32[8,256]{1,0:T(8,128)}, u32[]{:S(2)}) copy-start(f32[8,256]{1,0:T(8,128)} %constant.26.clone.sg_ref) | copy-start | bytes 24580
  26.3 10.2 %collective-permute-start.4 = (f32[33,512]{1,0:T(8,128)S(1)}, f32[33,512]{1,0:T(8,128)S(1)}, u32[]{:S(2)}, u32[]{:S(2)}) collective-permute-start(f32[33,512]{1,0:T(8,128)S(1)} %get-tuple-element.49), channel_id=1, source_target_pairs={{0,4},{4,0},{8,12},{12,8},{16,20},{20,16},{24,28},{28,24},{32,36},... | collective-permute-start | bytes 202760 | tf_op jit(solution)/shard_map/ppermute | solution.py:553
  26.4 10.1 %collective-permute-start.5 = (f32[33,512]{1,0:T(8,128)S(1)}, f32[33,512]{1,0:T(8,128)S(1)}, u32[]{:S(2)}, u32[]{:S(2)}) collective-permute-start(f32[33,512]{1,0:T(8,128)S(1)} %get-tuple-element.50), channel_id=1, source_target_pairs={{0,252},{4,8},{8,4},{12,16},{16,12},{20,24},{24,20},{28,32},{32,28... | collective-permute-start | bytes 202760 | tf_op jit(solution)/shard_map/ppermute | solution.py:554
  30.1 6.4 %collective-permute-start.6 = (f32[40,256]{1,0:T(8,128)S(1)}, f32[40,256]{1,0:T(8,128)S(1)}, u32[]{:S(2)}, u32[]{:S(2)}) collective-permute-start(f32[40,256]{1,0:T(8,128)S(1)} %get-tuple-element.51), channel_id=1, source_target_pairs={{0,1},{1,0},{2,3},{3,2},{4,5},{5,4},{6,7},{7,6},{8,9},{9,8},{10,11... | collective-permute-start | bytes 122888 | tf_op jit(solution)/shard_map/ppermute | solution.py:555
  32.5 4.1 %collective-permute-start.7 = (f32[40,256]{1,0:T(8,128)S(1)}, f32[40,256]{1,0:T(8,128)S(1)}, u32[]{:S(2)}, u32[]{:S(2)}) collective-permute-start(f32[40,256]{1,0:T(8,128)S(1)} %get-tuple-element.52), channel_id=1, source_target_pairs={{0,3},{1,2},{2,1},{3,0},{4,7},{5,6},{6,5},{7,4},{8,11},{9,10},{10,... | collective-permute-start | bytes 122888 | tf_op jit(solution)/shard_map/ppermute | solution.py:556
  33.7 2.9 %copy-start.3 = (bf16[768,512]{1,0:T(8,128)(2,1)S(1)}, bf16[768,512]{1,0:T(8,128)(2,1)}, u32[]{:S(2)}) copy-start(bf16[768,512]{1,0:T(8,128)(2,1)} %constant.29.clone.pv_ref) | copy-start | bytes 2359300
  39.2 21.4 %copy-start.2 = (f32[40,2,625]{2,1,0:T(2,128)S(1)}, f32[40,2,625]{2,1,0:T(2,128)}, u32[]{:S(2)}) copy-start(f32[40,2,625]{2,1,0:T(2,128)} %refs_2_.1) | copy-start | bytes 600004
